TPU v7x, 32 devices: a whole 2x2x4 slice. The times are simulated.
32 devices in a mesh: hist: 16 (over z, x, core), orb: 2 (over y).
Axes of the slice: x: 2, y: 2, z: 4, core: 2. Of those that a mesh axis runs over, the one named last changes fastest.
Arguments:
- g_hist: bfloat16 [32, 64, 2048], P('hist', 'orb'), may hold values from -6 to 6
- sigma_hist: bfloat16 [2, 64, 2048], P(None, None, 'hist'), may hold values from -0.125 to 0.125
- diag_inv: float32 [32, 64, 64], P('hist'), may hold values from -0.75 to 0.75
- previous: float32 [2, 32, 64, 64], P(None, 'hist', 'orb'), may hold values from -6 to 6
- block_of_slot: int32 [16], replicated, may hold values from 0 to 15, each once
- front_pos: int32 [2], replicated, may hold values from 16 to 31
Outputs:
- g_row: float32 [2, 32, 64, 64], P(None, 'hist', 'orb')
- sigma_row: float32 [2, 32, 64, 64], P(None, 'hist', 'orb')
Inputs may be any that keep to these rules, and one draw needn't show every extreme that they name: `block_of_slot`: every block index appears once.
All inputs are finite; a program needn't handle non-finite values.
Results may differ from a plain program's by a relative error of at most 0.0003.
Values may be sent and summed in bfloat16 or wider, within the bound.
A program may use at most 64 MiB of HBM per device.

v0:
```python
import jax
import jax.numpy as jnp
from jax import lax
from jax.sharding import PartitionSpec as P

COUPLING = 0.5


def broadcast(value, axis, root):
    mine = lax.axis_index(axis) == root
    return lax.psum(jnp.where(mine, value, jnp.zeros_like(value)), axis)


def contract(g_piece, s_piece, times, col_time, front_pos):
    g_kept = jnp.where(
        (times[None, :] >= col_time[:, None])[:, None, :], g_piece, jnp.zeros_like(g_piece)
    )
    s_kept = jnp.where(
        (times[None, :] <= front_pos[:, None])[:, None, :], s_piece, jnp.zeros_like(s_piece)
    )
    return jnp.einsum("tcx,fax->ftca", g_kept, s_kept, preferred_element_type=jnp.float32)


def inverse_row(diag_inv, when, col_count):
    local = lax.dynamic_index_in_dim(diag_inv, when % col_count, 0, keepdims=False)
    return broadcast(local, "hist", when // col_count)


def body(g_hist, sigma_hist, diag_inv, previous, block_of_slot, front_pos):
    col_count = g_hist.shape[0]
    half_cols = g_hist.shape[1]
    orb_width = sigma_hist.shape[1]
    orb_id = lax.axis_index("orb")
    slot_id = lax.axis_index("hist")
    my_block = lax.dynamic_index_in_dim(block_of_slot, slot_id, 0, keepdims=False)
    col_time = my_block * col_count + jnp.arange(col_count, dtype=jnp.int32)
    piece = lax.all_gather(sigma_hist, "hist", axis=2, tiled=True)
    count = piece.shape[2]
    times = jnp.arange(count, dtype=jnp.int32) // orb_width
    integral = contract(g_hist, piece, times, col_time, front_pos)
    combined = previous + integral
    rows = jnp.stack([inverse_row(diag_inv, front_pos[front], col_count) for front in range(2)])
    g_row = jnp.einsum("ftcb,fab->ftca", combined, rows, precision=lax.Precision.HIGHEST)
    whole = lax.all_gather(g_row, "orb", axis=2, tiled=True)
    mirror = jnp.swapaxes(lax.dynamic_slice_in_dim(whole, orb_id * half_cols, half_cols, 3), 2, 3)
    sigma_row = COUPLING * g_row * g_row * mirror
    return (g_row, sigma_row)


def solution(mesh):
    in_specs = (
        P("hist", "orb", None),
        P(None, None, "hist"),
        P("hist", None, None),
        P(None, "hist", "orb", None),
        P(),
        P(),
    )
    out_specs = (P(None, "hist", "orb", None), P(None, "hist", "orb", None))
    return jax.shard_map(body, mesh=mesh, in_specs=in_specs, out_specs=out_specs, check_vma=False)
```

profile of v0, /device:TPU:0, one launch (start us, length us, event | category | flops | bytes accessed | tf_op | source)
XLA Modules:
  0.0 99.1 jit_solution(8734970899965628988)
XLA Ops:
  0.6 0.0 copy-start.4
  0.6 0.0 copy-start.3
  0.6 25.0 %all_gather.6 = bf16[2,64,2048]{2,1,0:T(8,128)(2,1)S(1)} all-gather(bf16[2,64,128]{2,1,0:T(8,128)(2,1)} %param.7), channel_id=1, replica_groups=mesh['hist'=16,'orb'=2] {'hist'}, dimensions={2}, use_global_device_ids=true | all-gather | bytes 557056 | tf_op jit(solution)/shard_map/all_gather | solution.py:37
  25.6 0.0 copy-start.5
  25.6 0.7 copy-done.5
  26.3 0.6 dynamic_slice.14
  27.5 0.0 copy-start.2
  27.5 0.6 copy-done.2
  28.2 0.1 broadcast_compare_fusion
  28.3 0.0 copy-done.4
  28.3 0.0 copy-done.3
  28.3 0.4 fusion
  28.7 0.0 copy-start.1
  28.7 0.6 fusion.18
  34.5 0.0 copy-done.1
  34.5 57.9 %all-reduce = (f32[1,64,64]{2,1,0:T(8,128)S(1)}, f32[1,64,64]{2,1,0:T(8,128)S(1)}) all-reduce(f32[1,64,64]{2,1,0:T(8,128)S(1)} %get-tuple-element.7, f32[1,64,64]{2,1,0:T(8,128)S(1)} %get-tuple-element.6), channel_id=1, replica_groups=mesh['hist'=16,'orb'=2] {'hist'}, use_global_device_ids=true, to_apply=%region_1.2 | all-reduce | flops 8192 | bytes 65536 | tf_op jit(solution)/shard_map/psum | solution.py:11
  92.4 0.2 fusion.10
  92.7 0.0 copy-start
  92.7 0.1 copy.8
  92.8 0.5 copy-done
  93.3 4.9 %all_gather.7 = f32[2,2,64,64]{3,2,1,0:T(8,128)S(1)} all-gather(f32[2,2,32,64]{3,2,1,0:T(8,128)S(1)} %fusion.10), channel_id=1, replica_groups=mesh['hist'=16,'orb'=2] {'orb'}, dimensions={2}, use_global_device_ids=true | all-gather | bytes 98304 | tf_op jit(solution)/shard_map/all_gather | solution.py:44
  98.2 0.1 fusion.8
  98.3 0.7 copy.10
  (3 shorter events, 0.0 us)
Async XLA Ops:
  0.6 27.6 %copy-start.4 = (f32[2,2,32,64]{3,2,1,0:T(8,128)S(1)}, f32[2,2,32,64]{3,2,1,0:T(8,128)}, u32[]{:S(2)}) copy-start(f32[2,2,32,64]{3,2,1,0:T(8,128)} %param.9) | copy-start | bytes 98308
  0.6 27.6 %copy-start.3 = (bf16[2,32,2048]{2,1,0:T(8,128)(2,1)S(1)}, bf16[2,32,2048]{2,1,0:T(8,128)(2,1)}, u32[]{:S(2)}) copy-start(bf16[2,32,2048]{2,1,0:T(8,128)(2,1)} %param.6) | copy-start | bytes 786436
  25.6 0.7 copy-start.5
  27.5 0.7 copy-start.2
  28.7 5.8 %copy-start.1 = (f32[2,64,64]{2,1,0:T(8,128)S(1)}, f32[2,64,64]{2,1,0:T(8,128)}, u32[]{:S(2)}) copy-start(f32[2,64,64]{2,1,0:T(8,128)} %param.8) | copy-start | bytes 98308
  92.7 0.6 copy-start
where the time goes:
time: 99.3 us; the launch traced here: 99.1 us
  blocking collectives  87.8 us (88%)
  between operations  6.62 us (7%)
  local copies, waits for them, and re-layouts  3.81 us (4%)
    psum x1, blocking collectives, broadcast(): return lax.psum(jnp.where(mine, value, jnp.zeros_like(value)), axis)  57.9 us
    all_gather x1, blocking collectives, body(): piece = lax.all_gather(sigma_hist, 'hist', axis=2, tiled=True)  25 us
    all_gather x1, blocking collectives, body(): whole = lax.all_gather(g_row, 'orb', axis=2, tiled=True)  4.92 us
    unnamed x13, local copies, waits for them, and re-layouts  2.55 us

commit v1 on v0

v1 whole, which is shorter than its diff:
```python
import functools

import jax
import jax.numpy as jnp
from jax import lax
from jax.experimental import pallas as pl
from jax.experimental.pallas import tpu as pltpu
from jax.sharding import PartitionSpec as P

COUPLING = 0.5
MESH = pl.DeviceIdType.MESH


def xor(a, b, size):
    out, bit = 0, 1
    while bit < size:
        out = out + bit * ((a // bit + b // bit) % 2)
        bit *= 2
    return out


def loop(low, high, step):
    if high - low <= 8:
        for i in range(low, high):
            step(i)
    else:
        lax.fori_loop(low, high, lambda i, c: (step(i), c)[1], 0)


def kernel(lines, blocks_ref, front_ref, g_hbm, s_hbm, d_hbm, p_hbm, g_out, s_out,
           g_v, all_s, d_v, p_v, acc, d_mine, d_core, d_x, d_z, d_part, d_all,
           t_send, t_recv, loc_sem, z_send, z_recv, x_send, x_recv, c_send, c_recv,
           d_send, d_recv, t_sems):
    cols, half = g_hbm.shape[0], g_hbm.shape[1]
    orb, lanes = s_hbm.shape[1], s_hbm.shape[2]
    me = lax.axis_index("hist")
    o = lax.axis_index("orb")
    core = me % 2
    xi = (me // 2) % 2
    z = me // 4
    quarter = orb // 4

    def at(zz, xx, cc):
        return (zz * 2 + xx) * 2 + cc

    core_peer = (at(z, xi, 1 - core), o)
    x_peer = (at(z, 1 - xi, core), o)
    y_peer = (me, 1 - o)
    yc_peer = (at(z, xi, 1 - core), 1 - o)

    def z_peer(d):
        return (at(xor(z, d, lines), xi, core), o)

    load_s = pltpu.make_async_copy(s_hbm, all_s.at[z, xi, core], loc_sem.at[0])
    load_d = pltpu.make_async_copy(d_hbm, d_v, loc_sem.at[1])
    load_g = pltpu.make_async_copy(g_hbm, g_v, loc_sem.at[2])
    load_p = pltpu.make_async_copy(p_hbm, p_v, loc_sem.at[3])
    load_s.start()
    load_d.start()
    load_g.start()
    load_p.start()

    barrier = pltpu.get_barrier_semaphore()

    def greet(peer):
        pl.semaphore_signal(barrier, inc=1, device_id=peer, device_id_type=MESH)

    loop(1, lines, lambda d: greet(z_peer(d)))
    for peer in (x_peer, core_peer, y_peer, yc_peer):
        greet(peer)
    pl.semaphore_wait(barrier, lines + 3)

    def send(src, dst, ssem, rsem, peer):
        return pltpu.make_async_remote_copy(
            src_ref=src, dst_ref=dst, send_sem=ssem, recv_sem=rsem,
            device_id=peer, device_id_type=MESH)

    def piece(d, xx, cc):
        return all_s.at[xor(z, d, lines), xx, cc]

    def z_copy(d):
        return send(piece(0, xi, core), piece(0, xi, core), z_send.at[d], z_recv.at[d], z_peer(d))

    def x_copy(d):
        return send(piece(d, xi, core), piece(d, xi, core), x_send.at[d], x_recv.at[d], x_peer)

    def c_copy(d, other):
        xx = xi + other - 2 * xi * other
        k = other * lines + d
        return send(piece(d, xx, core), piece(d, xx, core), c_send.at[k], c_recv.at[k], core_peer)

    load_s.wait()
    loop(1, lines, lambda d: z_copy(lines - d).start())
    x_copy(0).start()
    c_copy(0, 0).start()

    load_d.wait()

    def rows_of(q):
        part = []
        for f in range(2):
            when = front_ref[f]
            mine = (when // cols) == me
            got = d_v[when % cols, pl.ds(pl.multiple_of(q * quarter, 8), quarter), :]
            part.append(jnp.where(mine, got, jnp.zeros_like(got)))
        return jnp.concatenate(part, axis=1)

    my_q = o * 2 + core
    d_mine[...] = rows_of(o * 2 + 1 - core)
    d_c = send(d_mine, d_core, d_send.at[0], d_recv.at[0], core_peer)
    d_c.start()
    own_rows = rows_of(my_q)
    load_g.wait()
    acc[...] = jnp.zeros_like(acc)

    col0 = blocks_ref[me] * cols

    def product(d, xx):
        chip = xor(z, d, lines) * 2 + xx
        width = 2 * lanes
        start = pl.multiple_of(chip * width, width)
        time = (lax.broadcasted_iota(jnp.int32, (1, width), 1) + start) // orb
        one, zero = jnp.float32(1), jnp.float32(0)
        left = jnp.concatenate(
            [g_v[t, :, pl.ds(start, width)]
             * jnp.where(time >= col0 + t, one, zero).astype(jnp.bfloat16)
             for t in range(cols)], axis=0)
        zz = xor(z, d, lines)
        both = jnp.concatenate([all_s[zz, xx, 0], all_s[zz, xx, 1]], axis=2)
        right = jnp.concatenate(
            [both[f] * jnp.where(time <= front_ref[f], one, zero).astype(jnp.bfloat16)
             for f in range(2)], axis=0)
        acc[...] += lax.dot_general(left, right, (((1,), (1,)), ((), ())),
                                    preferred_element_type=jnp.float32)

    d_c.wait()
    d_x[0] = own_rows + d_core[...]
    d_xc = send(d_x.at[0], d_x.at[1], d_send.at[1], d_recv.at[1], x_peer)
    d_xc.start()

    def relay(d):
        z_copy(d).wait_recv()
        x_copy(d).start()
        c_copy(d, 0).start()

    relay(1)
    d_xc.wait()
    d_z[0] = d_x[0] + d_x[1]

    def dz_copy(d):
        return send(d_z.at[0], d_z.at[d], d_send.at[5 + d], d_recv.at[5 + d], z_peer(d))

    loop(1, lines, lambda d: dz_copy(d).start())
    loop(2, lines, relay)

    c_copy(0, 0).wait_recv()
    product(0, xi)

    def relay_x(d):
        x_copy(d).wait_recv()
        c_copy(d, 1).start()

    def near(d):
        relay_x(d - 1)
        c_copy(d, 0).wait_recv()
        product(d, xi)

    loop(1, lines, near)

    loop(1, lines, lambda d: dz_copy(d).wait())
    total = d_z[0]
    total = lax.fori_loop(1, lines, lambda d, t: t + d_z[d], total)
    d_part[...] = total
    outs = [send(d_part, d_all.at[my_q], d_send.at[2 + k], d_recv.at[2 + k], peer)
            for k, peer in enumerate((core_peer, y_peer, yc_peer))]
    for c in outs:
        c.start()
    d_all[my_q] = total
    relay_x(lines - 1)

    def far(d):
        c_copy(d, 1).wait_recv()
        product(d, 1 - xi)

    loop(0, lines, far)

    load_p.wait()
    prev = jnp.concatenate([p_v[f].reshape(cols * half, orb) for f in range(2)], axis=1)
    combined = acc[...] + prev
    for c in outs:
        c.wait()
    rows = d_all[...].reshape(orb, 2 * orb)
    lane = lax.broadcasted_iota(jnp.int32, rows.shape, 1)
    none = jnp.zeros_like(rows)
    weight = jnp.concatenate(
        [jnp.where(lane < orb, rows, none), jnp.where(lane < orb, none, rows)], axis=0)
    contract = (((1,), (1,)), ((), ()))
    flipped = lax.dot_general(weight, combined, contract, precision=lax.Precision.HIGHEST,
                              preferred_element_type=jnp.float32)

    def block(which):
        parts = []
        for f in range(2):
            low = flipped[f * orb:f * orb + half]
            high = flipped[f * orb + half:f * orb + 2 * half]
            parts.append(jnp.where(which == 0, low, high))
        return jnp.concatenate(parts, axis=1)

    t_send[...] = block(1 - o)
    t_copy = send(t_send, t_recv, t_sems.at[0], t_sems.at[1], y_peer)
    t_copy.start()
    g_new = lax.dot_general(combined, weight, contract, precision=lax.Precision.HIGHEST,
                            preferred_element_type=jnp.float32)
    scaled = COUPLING * g_new * g_new
    own = block(o)
    for f in range(2):
        for t in range(cols):
            g_out[f, t] = g_new[t * half:(t + 1) * half, f * orb:(f + 1) * orb]
    t_copy.wait()
    other = t_recv[...]
    first = jnp.where(o == 0, own, other)
    second = jnp.where(o == 0, other, own)
    for f in range(2):
        for t in range(cols):
            k = (f * cols + t) * half
            mirror = jnp.concatenate([first[:, k:k + half], second[:, k:k + half]], axis=1)
            s_out[f, t] = scaled[t * half:(t + 1) * half, f * orb:(f + 1) * orb] * mirror

    loop(1, lines, lambda d: z_copy(d).wait_send())
    loop(0, lines, lambda d: x_copy(d).wait_send())
    loop(0, lines, lambda d: c_copy(d, 0).wait_send())
    loop(0, lines, lambda d: c_copy(d, 1).wait_send())


def body(lines, g_hist, sigma_hist, diag_inv, previous, block_of_slot, front_pos):
    cols, half, depth = g_hist.shape
    orb, lanes = sigma_hist.shape[1], sigma_hist.shape[2]
    quarter = orb // 4
    out = jax.ShapeDtypeStruct(previous.shape, jnp.float32)
    smem = pl.BlockSpec(memory_space=pltpu.SMEM)
    hbm = pl.BlockSpec(memory_space=pl.ANY)
    vmem = pl.BlockSpec(memory_space=pltpu.VMEM)
    dma = pltpu.SemaphoreType.DMA
    f32 = jnp.float32
    flops = 2 * cols * half * depth * 2 * orb
    return pl.pallas_call(
        functools.partial(kernel, lines),
        out_shape=(out, out),
        in_specs=[smem, smem, hbm, hbm, hbm, hbm],
        out_specs=(vmem, vmem),
        scratch_shapes=[
            pltpu.VMEM(g_hist.shape, g_hist.dtype),
            pltpu.VMEM((lines, 2, 2) + sigma_hist.shape, sigma_hist.dtype),
            pltpu.VMEM(diag_inv.shape, f32),
            pltpu.VMEM(previous.shape, f32),
            pltpu.VMEM((cols * half, 2 * orb), f32),
            pltpu.VMEM((quarter, 2 * orb), f32),
            pltpu.VMEM((quarter, 2 * orb), f32),
            pltpu.VMEM((2, quarter, 2 * orb), f32),
            pltpu.VMEM((lines, quarter, 2 * orb), f32),
            pltpu.VMEM((quarter, 2 * orb), f32),
            pltpu.VMEM((4, quarter, 2 * orb), f32),
            pltpu.VMEM((half, 2 * cols * half), f32),
            pltpu.VMEM((half, 2 * cols * half), f32),
            dma((4,)),
            dma((lines,)), dma((lines,)),
            dma((lines,)), dma((lines,)),
            dma((2 * lines,)), dma((2 * lines,)),
            dma((5 + lines,)), dma((5 + lines,)),
            dma((2,)),
        ],
        compiler_params=pltpu.CompilerParams(collective_id=0, has_side_effects=True),
        cost_estimate=pl.CostEstimate(flops=flops, bytes_accessed=2 * g_hist.size, transcendentals=0),
    )(block_of_slot, front_pos, g_hist, sigma_hist, diag_inv, previous)


def solution(mesh):
    lines = mesh.shape["hist"] // 4
    in_specs = (
        P("hist", "orb", None),
        P(None, None, "hist"),
        P("hist", None, None),
        P(None, "hist", "orb", None),
        P(),
        P(),
    )
    out_specs = (P(None, "hist", "orb", None), P(None, "hist", "orb", None))
    return jax.shard_map(functools.partial(body, lines), mesh=mesh, in_specs=in_specs,
                         out_specs=out_specs, check_vma=False)
```

time: 99.3 us -> 23.7 us (0.24)
  blocking collectives: 87.8 us -> 0 us
  Pallas kernels: 0 us -> 20.8 us
  between operations: 6.62 us -> 0.65 us
  local copies, waits for them, and re-layouts: 3.81 us -> 2.14 us
    psum x1 -> x0, blocking collectives: 57.9 us -> none  [broadcast(): return lax.psum(jnp.where(mine, value, jnp.zeros_like(value)), axis)]
    all_gather x2 -> x0, blocking collectives: 29.9 us -> none  [the longest x1 25 us: body(): piece = lax.all_gather(sigma_hist, 'hist', axis=2, tiled=True)]
    pallas_call x0 -> x1, Pallas kernels: none -> 20.8 us  [body(): pl.pallas_call(functools.partial(kernel, lines), out_shape=(out, out), in...]
    unnamed x13 -> x4, local copies, waits for them, and re-layouts: 2.55 us -> 2.14 us
where the time goes in v1:
time: 23.7 us; the launch traced here: 23.6 us
  Pallas kernels  20.8 us (88%)
  local copies, waits for them, and re-layouts  2.14 us (9%)
  between operations  0.65 us (3%)
    pallas_call x1, Pallas kernels, body(): pl.pallas_call(functools.partial(kernel, lines), out_shape=(out, out), in...  20.8 us
    unnamed x4, local copies, waits for them, and re-layouts  2.14 us

profile of v1, /device:TPU:0, one launch (start us, length us, event | category | flops | bytes accessed | tf_op | source)
XLA Modules:
  0.0 23.6 jit_solution(5797462271332584354)
XLA Ops:
  0.6 20.8 %shard_map.77 = (f32[2,2,32,64]{3,2,1,0:T(8,128)}, f32[2,2,32,64]{3,2,1,0:T(8,128)}) custom-call(s32[16]{0:T(128)} %blocks_ref.1, s32[2]{0:T(128)} %front_ref.1, bf16[2,32,2048]{2,1,0:T(8,128)(2,1)} %g_hbm.1, bf16[2,64,128]{2,1,0:T(8,128)(2,1)} %s_hbm.1, f32[2,64,64]{2,1,0:T(8,128)} %d_hbm.1, f32[2,2,32,64]{3,2,1,0:T(8,128)} %p_hbm.1), custom_call_target="tpu_custom_call" | custom-call | flops 33554432 | bytes 262144 | tf_op jit(solution)/shard_map/pallas_call | solution.py:246
  21.4 0.0 copy-start
  21.4 1.5 %copy.10 = f32[2,2,32,64]{3,2,1,0:T(8,128)} copy(f32[2,2,32,64]{3,2,1,0:T(8,128)} %get-tuple-element.4) | data formatting | bytes 65536
  22.9 0.0 copy-done
  22.9 0.6 %copy.11 = f32[2,2,32,64]{3,2,1,0:T(8,128)} copy(f32[2,2,32,64]{3,2,1,0:T(8,128)S(1)} %copy-done) | data formatting | bytes 65536
Async XLA Ops:
  21.4 1.5 %copy-start = (f32[2,2,32,64]{3,2,1,0:T(8,128)S(1)}, f32[2,2,32,64]{3,2,1,0:T(8,128)}, u32[]{:S(2)}) copy-start(f32[2,2,32,64]{3,2,1,0:T(8,128)} %get-tuple-element.5) | copy-start | bytes 98308

commit v2 on v1

v2 whole, which is shorter than its diff:
```python
import functools

import jax
import jax.numpy as jnp
from jax import lax
from jax.experimental import pallas as pl
from jax.experimental.pallas import tpu as pltpu
from jax.sharding import PartitionSpec as P

COUPLING = 0.5
MESH = pl.DeviceIdType.MESH


def xor(a, b, size):
    out, bit = 0, 1
    while bit < size:
        out = out + bit * ((a // bit + b // bit) % 2)
        bit *= 2
    return out


def loop(low, high, step):
    if high - low <= 8:
        for i in range(low, high):
            step(i)
    else:
        lax.fori_loop(low, high, lambda i, c: (step(i), c)[1], 0)


def kernel(lines, blocks_ref, front_ref, g_hbm, s_hbm, d_hbm, p_hbm, out,
           g_v, all_s, d_v, p_v, acc, d_out, d_in, d_z, d_all, packed,
           loc_sem, z_send, z_recv, x_send, x_recv, c_send, c_recv,
           d_send, d_recv, dz_send, dz_recv, y_send, y_recv):
    cols, half = g_hbm.shape[0], g_hbm.shape[1]
    orb, lanes = s_hbm.shape[1], s_hbm.shape[2]
    me = lax.axis_index("hist")
    o = lax.axis_index("orb")
    core = me % 2
    xi = (me // 2) % 2
    z = me // 4
    rows = orb // 2

    def at(zz, xx, cc):
        return (zz * 2 + xx) * 2 + cc

    core_peer = (at(z, xi, 1 - core), o)
    x_peer = (at(z, 1 - xi, core), o)
    xc_peer = (at(z, 1 - xi, 1 - core), o)
    y_peer = (me, 1 - o)

    def z_peer(d):
        return (at(xor(z, d, lines), xi, core), o)

    load_s = pltpu.make_async_copy(s_hbm.at[o], all_s.at[z, xi, core], loc_sem.at[0])
    load_d = pltpu.make_async_copy(d_hbm, d_v, loc_sem.at[1])
    load_g = pltpu.make_async_copy(g_hbm, g_v.at[o], loc_sem.at[2])
    load_p = pltpu.make_async_copy(p_hbm.at[o], p_v.at[o], loc_sem.at[3])
    load_s.start()
    load_d.start()
    load_g.start()
    load_p.start()

    barrier = pltpu.get_barrier_semaphore()

    def greet(peer):
        pl.semaphore_signal(barrier, inc=1, device_id=peer, device_id_type=MESH)

    loop(1, lines, lambda d: greet(z_peer(d)))
    for peer in (x_peer, xc_peer, core_peer, y_peer):
        greet(peer)

    def rows_of(part):
        when = front_ref[o]
        mine = (when // cols) == me
        first = pl.multiple_of(part * rows, 8)
        got = d_v[when % cols, pl.ds(first, rows), :]
        wide = jnp.concatenate([got[:rows // 2], got[rows // 2:]], axis=1)
        return jnp.where(mine, wide, jnp.zeros_like(wide))

    load_d.wait()
    d_out[0] = rows_of(core)
    d_out[1] = rows_of(1 - core)
    acc[...] = jnp.zeros_like(acc)
    load_s.wait()
    pl.semaphore_wait(barrier, lines + 3)

    def send(src, dst, ssem, rsem, peer):
        return pltpu.make_async_remote_copy(
            src_ref=src, dst_ref=dst, send_sem=ssem, recv_sem=rsem,
            device_id=peer, device_id_type=MESH)

    def piece(d, xx, cc):
        return all_s.at[xor(z, d, lines), xx, cc]

    def z_copy(d):
        return send(piece(0, xi, core), piece(0, xi, core), z_send.at[d], z_recv.at[d], z_peer(d))

    def x_copy(d):
        return send(piece(d, xi, core), piece(d, xi, core), x_send.at[d], x_recv.at[d], x_peer)

    def c_copy(d, other):
        xx = xi + other - 2 * xi * other
        k = other * lines + d
        return send(piece(d, xx, core), piece(d, xx, core), c_send.at[k], c_recv.at[k], core_peer)

    d_copies = [send(d_out.at[which], d_in.at[k], d_send.at[k], d_recv.at[k], peer)
                for k, (which, peer) in enumerate(((0, x_peer), (1, xc_peer), (1, core_peer)))]
    for c in d_copies:
        c.start()
    x_copy(0).start()
    loop(1, lines, lambda d: z_copy(lines - d).start())
    c_copy(0, 0).start()
    load_g.wait()
    g_copy = send(g_v.at[o], g_v.at[o], y_send.at[0], y_recv.at[0], y_peer)
    p_copy = send(p_hbm.at[1 - o], p_v.at[o], y_send.at[1], y_recv.at[1], y_peer)
    g_copy.start()
    p_copy.start()

    col0 = blocks_ref[me] * cols

    def product(d, xx):
        zz = xor(z, d, lines)
        width = 2 * lanes
        start = pl.multiple_of((zz * 2 + xx) * width, width)
        time = (lax.broadcasted_iota(jnp.int32, (1, width), 1) + start) // orb
        one, zero = jnp.float32(1), jnp.float32(0)
        left = []
        for t in range(cols):
            keep = jnp.where((time >= col0 + t) & (time <= front_ref[o]), one, zero)
            keep = keep.astype(jnp.bfloat16)
            left += [g_v[h, t, :, pl.ds(start, width)] * keep for h in range(2)]
        right = jnp.concatenate([all_s[zz, xx, 0], all_s[zz, xx, 1]], axis=1)
        acc[...] += lax.dot_general(jnp.concatenate(left, axis=0), right, (((1,), (1,)), ((), ())),
                                    preferred_element_type=jnp.float32)

    def relay(d):
        z_copy(d).wait_recv()
        x_copy(d).start()
        c_copy(d, 0).start()

    def relay_x(d):
        x_copy(d).wait_recv()
        c_copy(d, 1).start()

    def near(d):
        c_copy(d, 0).wait_recv()
        product(d, xi)

    def far(d):
        c_copy(d, 1).wait_recv()
        product(d, 1 - xi)

    def dz_copy(d):
        return send(d_z.at[0], d_z.at[d], dz_send.at[d], dz_recv.at[d], z_peer(d))

    relay_x(0)
    for c in d_copies:
        c.wait()
    d_z[0] = (d_out[0] + d_in[0]) + (d_in[1] + d_in[2])
    loop(1, lines, lambda d: dz_copy(d).start())
    loop(1, lines, relay)
    loop(1, lines - 1, relay_x)
    g_copy.wait_recv()
    near(0)
    near(1)
    relay_x(lines - 1)
    loop(1, lines, lambda d: dz_copy(d).wait())
    total = lax.fori_loop(1, lines, lambda d, t: t + d_z[d], d_z[0])
    d_all[core] = total
    d_last = send(d_all.at[core], d_all.at[core], d_send.at[3], d_recv.at[3], core_peer)
    d_last.start()
    loop(2, lines, near)
    loop(0, lines, far)

    load_p.wait()
    p_copy.wait()
    prev = jnp.concatenate([p_v[h, t] for t in range(cols) for h in range(2)], axis=0)
    combined = acc[...] + prev
    d_last.wait()
    weight = jnp.concatenate([d_all[c][:, k * orb:(k + 1) * orb]
                              for c in range(2) for k in range(2)], axis=0)
    contract = (((1,), (1,)), ((), ()))
    high = dict(precision=lax.Precision.HIGHEST, preferred_element_type=jnp.float32)
    flipped = lax.dot_general(weight, combined, contract, **high)
    g_new = lax.dot_general(combined, weight, contract, **high)
    t_copies = []
    for t in range(cols):
        g_t = g_new[t * orb:(t + 1) * orb]
        s_t = COUPLING * g_t * g_t * flipped[:, t * orb:(t + 1) * orb]
        done = jnp.concatenate([g_t, s_t], axis=1)
        packed[t] = jnp.where(o == 0, done[half:], done[:half])
        c = send(packed.at[t], out.at[o, t], y_send.at[2 + t], y_recv.at[2 + t], y_peer)
        c.start()
        t_copies.append(c)
        out[o, t] = jnp.where(o == 0, done[:half], done[half:])

    g_copy.wait_send()
    loop(1, lines, lambda d: z_copy(d).wait_send())
    loop(0, lines, lambda d: x_copy(d).wait_send())
    loop(0, lines, lambda d: c_copy(d, 0).wait_send())
    loop(0, lines, lambda d: c_copy(d, 1).wait_send())
    for c in t_copies:
        c.wait()


def body(lines, g_hist, sigma_hist, diag_inv, previous, block_of_slot, front_pos):
    cols, half, depth = g_hist.shape
    orb, lanes = sigma_hist.shape[1], sigma_hist.shape[2]
    smem = pl.BlockSpec(memory_space=pltpu.SMEM)
    hbm = pl.BlockSpec(memory_space=pl.ANY)
    dma = pltpu.SemaphoreType.DMA
    f32 = jnp.float32
    part = (orb // 4, 2 * orb)
    flops = 2 * cols * orb * depth * orb
    out = pl.pallas_call(
        functools.partial(kernel, lines),
        out_shape=pltpu.VMEM((2, cols, half, 2 * orb), f32),
        in_specs=[smem, smem, hbm, hbm, hbm, hbm],
        out_specs=pl.BlockSpec(memory_space=pltpu.VMEM),
        scratch_shapes=[
            pltpu.VMEM((2,) + g_hist.shape, g_hist.dtype),
            pltpu.VMEM((lines, 2, 2, orb, lanes), sigma_hist.dtype),
            pltpu.VMEM(diag_inv.shape, f32),
            pltpu.VMEM((2,) + previous.shape[1:], f32),
            pltpu.VMEM((cols * orb, orb), f32),
            pltpu.VMEM((2,) + part, f32),
            pltpu.VMEM((3,) + part, f32),
            pltpu.VMEM((lines,) + part, f32),
            pltpu.VMEM((2,) + part, f32),
            pltpu.VMEM((cols, half, 2 * orb), f32),
            dma((4,)),
            dma((lines,)), dma((lines,)),
            dma((lines,)), dma((lines,)),
            dma((2 * lines,)), dma((2 * lines,)),
            dma((4,)), dma((4,)),
            dma((lines,)), dma((lines,)),
            dma((2 + cols,)), dma((2 + cols,)),
        ],
        compiler_params=pltpu.CompilerParams(collective_id=0, has_side_effects=True),
        cost_estimate=pl.CostEstimate(flops=flops, bytes_accessed=2 * g_hist.size, transcendentals=0),
    )(block_of_slot, front_pos, g_hist, sigma_hist, diag_inv, previous)
    return out[..., :orb], out[..., orb:]


def solution(mesh):
    lines = mesh.shape["hist"] // 4
    in_specs = (
        P("hist", "orb", None),
        P(None, None, "hist"),
        P("hist", None, None),
        P(None, "hist", "orb", None),
        P(),
        P(),
    )
    out_specs = (P(None, "hist", "orb", None), P(None, "hist", "orb", None))
    return jax.shard_map(functools.partial(body, lines), mesh=mesh, in_specs=in_specs,
                         out_specs=out_specs, check_vma=False)
```

time: 23.7 us -> 20 us (0.84)
  Pallas kernels: 20.8 us -> 18.5 us
  local copies, waits for them, and re-layouts: 2.14 us -> 0.72 us
    pallas_call x1, Pallas kernels: 20.8 us -> 18.5 us  [body(): pl.pallas_call(functools.partial(kernel, lines), out_shape=pltpu.VMEM((2,...]
    unnamed x4 -> x0, local copies, waits for them, and re-layouts: 2.14 us -> none
    slice x0 -> x1, local copies, waits for them, and re-layouts: none -> 0.72 us  [body(): return (out[..., :orb], out[..., orb:])]
where the time goes in v2:
time: 20 us; the launch traced here: 19.8 us
  Pallas kernels  18.5 us (92%)
  local copies, waits for them, and re-layouts  0.72 us (4%)
  between operations  0.64 us (3%)
    pallas_call x1, Pallas kernels, body(): pl.pallas_call(functools.partial(kernel, lines), out_shape=pltpu.VMEM((2,...  18.5 us
    slice x1, local copies, waits for them, and re-layouts, body(): return (out[..., :orb], out[..., orb:])  0.72 us

profile of v2, /device:TPU:0, one launch (start us, length us, event | category | flops | bytes accessed | tf_op | source)
XLA Modules:
  0.0 19.8 jit_solution(11294096367925441126)
XLA Ops:
  0.6 18.5 %shard_map.77 = f32[2,2,32,128]{3,2,1,0:T(8,128)S(1)} custom-call(s32[16]{0:T(128)} %blocks_ref.1, s32[2]{0:T(128)} %front_ref.1, bf16[2,32,2048]{2,1,0:T(8,128)(2,1)} %g_hbm.1, bf16[2,64,128]{2,1,0:T(8,128)(2,1)} %s_hbm.1, f32[2,64,64]{2,1,0:T(8,128)} %d_hbm.1, f32[2,2,32,64]{3,2,1,0:T(8,128)} %p_hbm.1), custom_call_target="tpu_custom_call" | custom-call | flops 33554432 | bytes 262144 | tf_op jit(solution)/shard_map/pallas_call | solution.py:215
  19.1 0.7 %fusion = (f32[2,2,32,64]{3,2,1,0:T(8,128)}, f32[2,2,32,64]{3,2,1,0:T(8,128)}) fusion(f32[2,2,32,128]{3,2,1,0:T(8,128)S(1)} %shard_map.77), kind=kLoop, calls=%fused_computation | loop fusion | bytes 131072 | tf_op jit(solution)/shard_map/slice | solution.py:242

commit v3 on v2

--- a/solution.py
+++ b/solution.py
@@ -11,14 +11,6 @@
 MESH = pl.DeviceIdType.MESH
 
 
-def xor(a, b, size):
-    out, bit = 0, 1
-    while bit < size:
-        out = out + bit * ((a // bit + b // bit) % 2)
-        bit *= 2
-    return out
-
-
 def loop(low, high, step):
     if high - low <= 8:
         for i in range(low, high):
@@ -28,9 +20,9 @@
 
 
 def kernel(lines, blocks_ref, front_ref, g_hbm, s_hbm, d_hbm, p_hbm, out,
-           g_v, all_s, d_v, p_v, acc, d_out, d_in, d_z, d_all, packed,
-           loc_sem, z_send, z_recv, x_send, x_recv, c_send, c_recv,
-           d_send, d_recv, dz_send, dz_recv, y_send, y_recv):
+           g_v, all_s, d_v, p_v, acc, d_out, d_in, d_z, d_up, d_all, packed,
+           loc_sem, z_send, u_send, z_recv, x_send, x_recv, c_send, c_recv,
+           d_send, d_recv, dz_send, dz_recv, du_send, y_send, y_recv):
     cols, half = g_hbm.shape[0], g_hbm.shape[1]
     orb, lanes = s_hbm.shape[1], s_hbm.shape[2]
     me = lax.axis_index("hist")
@@ -48,8 +40,13 @@
     xc_peer = (at(z, 1 - xi, 1 - core), o)
     y_peer = (me, 1 - o)
 
-    def z_peer(d):
-        return (at(xor(z, d, lines), xi, core), o)
+    def z_peer(zz):
+        return (at(zz, xi, core), o)
+
+    not_top = z + 1 < lines
+
+    def source(j):
+        return jnp.where(j <= z, z - j, j)
 
     load_s = pltpu.make_async_copy(s_hbm.at[o], all_s.at[z, xi, core], loc_sem.at[0])
     load_d = pltpu.make_async_copy(d_hbm, d_v, loc_sem.at[1])
@@ -65,7 +62,16 @@
     def greet(peer):
         pl.semaphore_signal(barrier, inc=1, device_id=peer, device_id_type=MESH)
 
-    loop(1, lines, lambda d: greet(z_peer(d)))
+    @pl.when(z > 0)
+    def _():
+        greet(z_peer(z - 1))
+
+    def greet_above(d):
+        @pl.when(z + d < lines)
+        def _():
+            greet(z_peer(z + d))
+
+    loop(1, lines, greet_above)
     for peer in (x_peer, xc_peer, core_peer, y_peer):
         greet(peer)
 
@@ -82,34 +88,49 @@
     d_out[1] = rows_of(1 - core)
     acc[...] = jnp.zeros_like(acc)
     load_s.wait()
-    pl.semaphore_wait(barrier, lines + 3)
+    pl.semaphore_wait(barrier, 4 + z + jnp.where(not_top, 1, 0))
 
     def send(src, dst, ssem, rsem, peer):
         return pltpu.make_async_remote_copy(
             src_ref=src, dst_ref=dst, send_sem=ssem, recv_sem=rsem,
             device_id=peer, device_id_type=MESH)
 
-    def piece(d, xx, cc):
-        return all_s.at[xor(z, d, lines), xx, cc]
-
-    def z_copy(d):
-        return send(piece(0, xi, core), piece(0, xi, core), z_send.at[d], z_recv.at[d], z_peer(d))
-
-    def x_copy(d):
-        return send(piece(d, xi, core), piece(d, xi, core), x_send.at[d], x_recv.at[d], x_peer)
-
-    def c_copy(d, other):
-        xx = xi + other - 2 * xi * other
-        k = other * lines + d
-        return send(piece(d, xx, core), piece(d, xx, core), c_send.at[k], c_recv.at[k], core_peer)
+    def down_copy(d):
+        ref = all_s.at[z, xi, core]
+        return send(ref, ref, z_send.at[d], z_recv.at[z], z_peer(z - d))
+
+    def up_copy(src):
+        ref = all_s.at[src, xi, core]
+        return send(ref, ref, u_send.at[src], z_recv.at[src], z_peer(z + 1))
+
+    def x_copy(src):
+        ref = all_s.at[src, xi, core]
+        return send(ref, ref, x_send.at[src], x_recv.at[src], x_peer)
+
+    def c_copy(src, other):
+        ref = all_s.at[src, xi + other - 2 * xi * other, core]
+        k = other * lines + src
+        return send(ref, ref, c_send.at[k], c_recv.at[k], core_peer)
+
+    def below(act):
+        def step(d):
+            @pl.when(z >= d)
+            def _():
+                act(d)
+        return step
 
     d_copies = [send(d_out.at[which], d_in.at[k], d_send.at[k], d_recv.at[k], peer)
                 for k, (which, peer) in enumerate(((0, x_peer), (1, xc_peer), (1, core_peer)))]
     for c in d_copies:
         c.start()
-    x_copy(0).start()
-    loop(1, lines, lambda d: z_copy(lines - d).start())
-    c_copy(0, 0).start()
+    loop(1, lines, lambda d: below(lambda e: down_copy(e).start())(lines - d))
+
+    @pl.when(not_top)
+    def _():
+        up_copy(z).start()
+
+    x_copy(z).start()
+    c_copy(z, 0).start()
     load_g.wait()
     g_copy = send(g_v.at[o], g_v.at[o], y_send.at[0], y_recv.at[0], y_peer)
     p_copy = send(p_hbm.at[1 - o], p_v.at[o], y_send.at[1], y_recv.at[1], y_peer)
@@ -118,8 +139,7 @@
 
     col0 = blocks_ref[me] * cols
 
-    def product(d, xx):
-        zz = xor(z, d, lines)
+    def product(zz, xx):
         width = 2 * lanes
         start = pl.multiple_of((zz * 2 + xx) * width, width)
         time = (lax.broadcasted_iota(jnp.int32, (1, width), 1) + start) // orb
@@ -133,40 +153,73 @@
         acc[...] += lax.dot_general(jnp.concatenate(left, axis=0), right, (((1,), (1,)), ((), ())),
                                     preferred_element_type=jnp.float32)
 
-    def relay(d):
-        z_copy(d).wait_recv()
-        x_copy(d).start()
-        c_copy(d, 0).start()
-
-    def relay_x(d):
-        x_copy(d).wait_recv()
-        c_copy(d, 1).start()
-
-    def near(d):
-        c_copy(d, 0).wait_recv()
-        product(d, xi)
-
-    def far(d):
-        c_copy(d, 1).wait_recv()
-        product(d, 1 - xi)
+    def relay(j):
+        src = source(j)
+        up_copy(src).wait_recv()
+
+        @pl.when((j <= z) & not_top)
+        def _():
+            up_copy(src).start()
+
+        x_copy(src).start()
+        c_copy(src, 0).start()
+
+    def relay_x(j):
+        src = source(j)
+        x_copy(src).wait_recv()
+        c_copy(src, 1).start()
+
+    def near(j):
+        src = source(j)
+        c_copy(src, 0).wait_recv()
+        product(src, xi)
+
+    def far(j):
+        src = source(j)
+        c_copy(src, 1).wait_recv()
+        product(src, 1 - xi)
 
     def dz_copy(d):
-        return send(d_z.at[0], d_z.at[d], dz_send.at[d], dz_recv.at[d], z_peer(d))
+        return send(d_z.at[z], d_z.at[z], dz_send.at[d], dz_recv.at[z], z_peer(z - d))
+
+    def dz_got(src):
+        return send(d_z.at[src], d_z.at[src], dz_send.at[0], dz_recv.at[src], x_peer)
+
+    dz_up = send(d_up, d_z.at[z], du_send, dz_recv.at[z], z_peer(z + 1))
 
     relay_x(0)
     for c in d_copies:
         c.wait()
-    d_z[0] = (d_out[0] + d_in[0]) + (d_in[1] + d_in[2])
-    loop(1, lines, lambda d: dz_copy(d).start())
-    loop(1, lines, relay)
+    here = (d_out[0] + d_in[0]) + (d_in[1] + d_in[2])
+    d_z[z] = here
+    d_up[...] = here
+    loop(1, lines, lambda d: below(lambda e: dz_copy(e).start())(lines - d))
+    relay(1)
+
+    @pl.when(z > 0)
+    def _():
+        dz_got(z - 1).wait_recv()
+        d_up[...] = here + d_z[z - 1]
+
+    @pl.when(not_top)
+    def _():
+        dz_up.start()
+
+    loop(2, lines, relay)
     loop(1, lines - 1, relay_x)
     g_copy.wait_recv()
     near(0)
     near(1)
     relay_x(lines - 1)
-    loop(1, lines, lambda d: dz_copy(d).wait())
-    total = lax.fori_loop(1, lines, lambda d, t: t + d_z[d], d_z[0])
-    d_all[core] = total
+    d_all[core] = d_up[...]
+
+    def gather_above(src):
+        @pl.when(src > z)
+        def _():
+            dz_got(src).wait_recv()
+            d_all[core] = d_all[core] + d_z[src]
+
+    loop(1, lines, gather_above)
     d_last = send(d_all.at[core], d_all.at[core], d_send.at[3], d_recv.at[3], core_peer)
     d_last.start()
     loop(2, lines, near)
@@ -195,7 +248,19 @@
         out[o, t] = jnp.where(o == 0, done[:half], done[half:])
 
     g_copy.wait_send()
-    loop(1, lines, lambda d: z_copy(d).wait_send())
+    def wait_above(src):
+        @pl.when((src <= z) & not_top)
+        def _():
+            up_copy(src).wait_send()
+
+    loop(0, lines, wait_above)
+    loop(1, lines, below(lambda d: down_copy(d).wait_send()))
+    loop(1, lines, below(lambda d: dz_copy(d).wait_send()))
+
+    @pl.when(not_top)
+    def _():
+        dz_up.wait_send()
+
     loop(0, lines, lambda d: x_copy(d).wait_send())
     loop(0, lines, lambda d: c_copy(d, 0).wait_send())
     loop(0, lines, lambda d: c_copy(d, 1).wait_send())
@@ -226,14 +291,15 @@
             pltpu.VMEM((2,) + part, f32),
             pltpu.VMEM((3,) + part, f32),
             pltpu.VMEM((lines,) + part, f32),
+            pltpu.VMEM(part, f32),
             pltpu.VMEM((2,) + part, f32),
             pltpu.VMEM((cols, half, 2 * orb), f32),
             dma((4,)),
-            dma((lines,)), dma((lines,)),
+            dma((lines,)), dma((lines,)), dma((lines,)),
             dma((lines,)), dma((lines,)),
             dma((2 * lines,)), dma((2 * lines,)),
             dma((4,)), dma((4,)),
-            dma((lines,)), dma((lines,)),
+            dma((lines,)), dma((lines,)), dma(()),
             dma((2 + cols,)), dma((2 + cols,)),
         ],
         compiler_params=pltpu.CompilerParams(collective_id=0, has_side_effects=True),

time: 20 us -> 22.4 us (1.12)
  the two profiles are of different devices: /device:TPU:0 before, /device:TPU:24 now
where the time goes in v3:
time: 22.4 us; the launch traced here: 22.2 us
  Pallas kernels  20.9 us (93%)
  local copies, waits for them, and re-layouts  0.72 us (3%)
  between operations  0.64 us (3%)
    pallas_call x1, Pallas kernels, body(): pl.pallas_call(functools.partial(kernel, lines), out_shape=pltpu.VMEM((2,...  20.9 us
    slice x1, local copies, waits for them, and re-layouts, body(): return (out[..., :orb], out[..., orb:])  0.72 us

profile of v3, /device:TPU:24, one launch (start us, length us, event | category | flops | bytes accessed | tf_op | source)
XLA Modules:
  0.0 22.2 jit_solution(13690686208983273758)
XLA Ops:
  0.6 20.9 %shard_map.77 = f32[2,2,32,128]{3,2,1,0:T(8,128)S(1)} custom-call(s32[16]{0:T(128)} %blocks_ref.1, s32[2]{0:T(128)} %front_ref.1, bf16[2,32,2048]{2,1,0:T(8,128)(2,1)} %g_hbm.1, bf16[2,64,128]{2,1,0:T(8,128)(2,1)} %s_hbm.1, f32[2,64,64]{2,1,0:T(8,128)} %d_hbm.1, f32[2,2,32,64]{3,2,1,0:T(8,128)} %p_hbm.1), custom_call_target="tpu_custom_call" | custom-call | flops 33554432 | bytes 262144 | tf_op jit(solution)/shard_map/pallas_call | solution.py:280
  21.5 0.7 %fusion = (f32[2,2,32,64]{3,2,1,0:T(8,128)}, f32[2,2,32,64]{3,2,1,0:T(8,128)}) fusion(f32[2,2,32,128]{3,2,1,0:T(8,128)S(1)} %shard_map.77), kind=kLoop, calls=%fused_computation | loop fusion | bytes 131072 | tf_op jit(solution)/shard_map/slice | solution.py:308
